TPU v7x, 128 devices: a whole 4x4x4 slice. The times are simulated.
128 devices in a mesh: pts: 16 (over z_hi, x, core), wlk: 8 (over z_lo, y).
Axes of the slice: x: 4, y: 4, z: 4 (z_hi: 2, z_lo: 2; z = z_hi * 2 + z_lo), core: 2. Of those that a mesh axis runs over, the one named last changes fastest.
Arguments:
- green_half: bfloat16 [16, 400, 2400], P('wlk'), may hold values from -6 to 6
- collocation: bfloat16 [2400, 9600], P('wlk', 'pts'), may hold values from -0.125 to 0.125
- occupied: bfloat16 [9600, 400], P('pts'), may hold values from -0.0029296875 to 0.0029296875
- kernel: bfloat16 [9600, 9600], P('pts'), may hold values from 0 to 16, as said below
Outputs:
- potential: float32 [16, 9600], P('wlk', 'pts')
- coulomb_energy: float32 [16], P('wlk')
- exchange_energy: float32 [16], P('wlk')
Inputs may be any that keep to these rules, and one draw needn't show every extreme that they name: kernel is symmetric and positive definite: kernel[p, q] equals kernel[q, p].
All inputs are finite; a program needn't handle non-finite values.
Results may differ from a plain program's by a relative error of at most 0.008.
Values may be sent and summed in bfloat16 or wider, within the bound.
A program may use at most 192 MiB of HBM per device.

v0:
```python
import jax
import jax.numpy as jnp
from jax import lax
from jax.experimental import pallas as pl
from jax.experimental.pallas import tpu as pltpu
from jax.sharding import PartitionSpec as P

MESH = pl.DeviceIdType.MESH
F32, BF16 = jnp.float32, jnp.bfloat16

ELEC = 400
PTS = 600
PAD = 640
ROWS = 608
DEEP = 300
DEEP_PAD = 304
GROUPS = 8
C_CUT = 160
KCH = 160
CHUNK = ((0, 256), (256, 256), (512, 128))
PARTS = range(len(CHUNK))
STEPS = ((0, 2), (2, 4), (4, 5))
FLOWS = 144


def dot(a, b):
    return jnp.dot(a, b, preferred_element_type=F32)


def body(green, colloc, occ, kmat, pot_out, sum_out,
         cin, oin, gv, g8, kst, kb, cbuf, acc, ttown, ttbuf, tp, op, otown, otbuf,
         trans, dens, dbuf, ebuf, exch, pot, local_sem, send, recv, d_send, d_recv, e_send, e_recv, hear):
    a, g = lax.axis_index("pts"), lax.axis_index("wlk")
    zh, x, c = a // 8, (a // 2) % 4, a % 2
    zl, y = g // 4, g % 4
    z = zh * 2 + zl
    is_same = zh == zl
    is_cross = zh != zl
    same = is_same.astype(jnp.int32)

    def at(zz, xx, cc, yy):
        return {"pts": (zz // 2) * 8 + xx * 2 + cc, "wlk": (zz % 2) * 4 + yy}

    sib = at(z, x, 1 - c, y)
    right, left = at(z, (x + 1) % 4, c, y), at(z, (x + 3) % 4, c, y)
    up, down = at(z, x, c, (y + 1) % 4), at(z, x, c, (y + 3) % 4)
    zmate = at(zh * 2 + 1 - zl, x, c, y)
    xmate = at(3 - z, x, c, y)
    lanes = tuple(pl.ds(pl.multiple_of(2 * start + c * size, 128), size) for start, size in CHUNK)
    cols = tuple(pl.ds(start, size) for start, size in CHUNK)
    numbers = iter(range(FLOWS))

    def flow(src, dst, dev):
        f = next(numbers)
        return pltpu.make_async_remote_copy(
            src_ref=src, dst_ref=dst, send_sem=send.at[f], recv_sem=recv.at[f],
            device_id=dev, device_id_type=MESH)

    def start(*copies):
        for cp in copies:
            cp.start()

    load_c = pltpu.make_async_copy(colloc, cin, local_sem.at[0])
    load_o = pltpu.make_async_copy(occ, oin, local_sem.at[1])
    load_g = [pltpu.make_async_copy(green.at[w], gv.at[pl.ds(w * ELEC, ELEC)], local_sem.at[2 + w]) for w in range(2)]
    pieces = [(s, min(KCH, PTS - s)) for s in range(0, PTS, KCH)]
    load_k = [pltpu.make_async_copy(kmat.at[pl.ds(s, n)], kst.at[i % 2, pl.ds(0, n)], local_sem.at[4 + i])
              for i, (s, n) in enumerate(pieces)]
    start(load_c, load_o)

    plane = z * 8 + x * 2 + c

    def plane_dev(r):
        q = (plane + r) % 32
        return at(q // 8, (q // 2) % 4, q % 2, y)

    barrier = pltpu.get_barrier_semaphore()
    for dev in (up, down, right, left, zmate, xmate, sib):
        pl.semaphore_signal(barrier, inc=1, device_id=dev, device_id_type=MESH)

    rounds = ((right, left), (right, left), (zmate, xmate), (sib,))

    def tell(r):
        for dev in rounds[r]:
            pl.semaphore_signal(hear.at[r], inc=1, device_id=dev, device_id_type=MESH)

    def heard(r):
        pl.semaphore_wait(hear.at[r], len(rounds[r]))
        if r + 1 < len(rounds):
            tell(r + 1)
    cbuf[g, :, pl.ds(PAD - 128, 128)] = jnp.zeros((DEEP_PAD, 128), BF16)
    cbuf[g, pl.ds(DEEP_PAD - 16, 16), :] = jnp.zeros((16, PAD), BF16)
    load_c.wait()
    cbuf[g, pl.ds(0, DEEP), pl.ds(0, PTS)] = cin[...]
    start(*load_g)
    load_o.wait()
    otown[:, pl.ds(PAD - 128, 128)] = jnp.zeros((ELEC, 128), BF16)
    otown[:, pl.ds(0, PTS)] = oin[...]

    @pl.when(is_same)
    def _():
        for h in PARTS:
            otbuf[0, :, lanes[h]] = otown[:, cols[h]]

    pl.semaphore_wait(barrier, 7)
    tell(0)

    def slot(zlo, yy):
        return zlo * 4 + yy

    def c_flow(k, h, dev, first=0, count=DEEP_PAD):
        ref = cbuf.at[k, pl.ds(first, count), cols[h]]
        return flow(ref, ref, dev)

    own_k, mate_k = slot(zl, y), slot(1 - zl, y)
    dn, un, on = (y + 3) % 4, (y + 1) % 4, (y + 2) % 4
    c_z, c_own, c_mate, c_far, c_zfar = [], [], [], [], []
    for h in PARTS:
        c_z.append(c_flow(own_k, h, zmate))
        c_own.append((c_flow(own_k, h, up), c_flow(own_k, h, down)))
        c_mate.append((c_flow(mate_k, h, up), c_flow(mate_k, h, down)))
        c_far.append((c_flow(slot(zl, dn), h, up, 0, C_CUT),
                      c_flow(slot(zl, un), h, down, C_CUT, DEEP_PAD - C_CUT)))
        c_zfar.append(c_flow(slot(zl, on), h, zmate))
    for h in PARTS:
        start(*c_own[h], c_z[h])

    def o_block(i, h):
        return otbuf.at[i, :, lanes[h]]

    o_xx = [flow(otown.at[:, cols[h]], o_block(0, h), xmate) for h in PARTS]
    o_right = [flow(o_block(0, h), o_block(1, h), right) for h in PARTS]
    o_left = [flow(o_block(0, h), o_block(2, h), left) for h in PARTS]
    o_sib = [flow(o_block(0, h), o_block(0, h), sib) for h in PARTS]
    o_far = [flow(o_block(1, 0), o_block(3, 0), right), flow(o_block(2, 1), o_block(3, 1), left),
             flow(o_block(1, 2), o_block(3, 2), right)]
    o_relay = [[flow(o_block(i, h), o_block(i, h), sib) for h in PARTS] for i in (1, 2, 3)]
    o_first = o_right + o_left + o_sib

    @pl.when(is_cross)
    def _():
        start(*o_xx)

    @pl.when(is_same)
    def _():
        for h in PARTS:
            start(o_right[h], o_left[h], o_sib[h])

    for cp in load_g:
        cp.wait()
    start(load_k[0], load_k[1])

    def cut_green(r, carry):
        rows = pl.ds(pl.multiple_of(r * 80, 16), 80)
        piece = gv[rows, :]
        for k in range(GROUPS):
            part = piece[:, k * DEEP:(k + 1) * DEEP]
            g8[k, rows, pl.ds(0, DEEP_PAD)] = jnp.concatenate([part, jnp.zeros((80, DEEP_PAD - DEEP), BF16)], axis=1)
        return carry

    lax.fori_loop(0, 10, cut_green, 0)
    heard(0)

    def add_theta(k, h, first=False):
        part = dot(g8[k, :, pl.ds(0, DEEP_PAD)], cbuf[k, :, cols[h]])
        if first:
            acc[:, cols[h]] = part
        else:
            acc[:, cols[h]] += part

    def cut_kernel(i):
        s, n = pieces[i]
        load_k[i].wait()

        def rows_at(r, carry):
            rows = pl.ds(pl.multiple_of(r * 16, 16), 16)
            out = pl.ds(pl.multiple_of(s + r * 16, 16), 16)
            for b in range(16):
                j, core = b // 2, b % 2
                kb[j, out, pl.ds(core * 256, 256)] = kst[i % 2, rows, pl.ds(b * PTS, 256)]
                kb[j, out, pl.ds(512 + core * 256, 256)] = kst[i % 2, rows, pl.ds(b * PTS + 256, 256)]
                part = kst[i % 2, rows, pl.ds(b * PTS + 512, PTS - 512)]
                kb[j, out, pl.ds(1024 + core * 128, 128)] = jnp.concatenate(
                    [part, jnp.zeros((16, PAD - PTS), BF16)], axis=1)
            return carry

        lax.fori_loop(0, (n + 15) // 16, rows_at, 0)
        if i + 2 < len(pieces):
            load_k[i + 2].start()

    def take(pair):
        for cp in pair:
            cp.wait_recv()

    def near_arrives(h):
        c_own[h][0].wait_recv()
        c_far[h][0].start()
        c_own[h][1].wait_recv()
        c_far[h][1].start()
        c_z[h].wait_recv()
        start(*c_mate[h])

    def far_arrives(h):
        take(c_far[h])
        c_zfar[h].start()

    for h in PARTS:
        add_theta(own_k, h, True)
    cut_kernel(0)
    heard(1)
    near_arrives(0)

    @pl.when(is_cross)
    def _():
        o_xx[0].wait_recv()
        start(o_right[0], o_left[0], o_sib[0])

    cut_kernel(1)
    near_arrives(1)
    near_arrives(2)
    heard(2)

    @pl.when(is_cross)
    def _():
        for h in (1, 2):
            o_xx[h].wait_recv()
            start(o_right[h], o_left[h], o_sib[h])

    def occupied_part(h):
        o_right[h].wait_recv()
        o_left[h].wait_recv()
        start(o_far[h], o_relay[0][h], o_relay[1][h])

    def occupied_goes_on():
        for h in PARTS:
            occupied_part(h)

    def add_near(h):
        add_theta(slot(zl, dn), h)
        add_theta(slot(zl, un), h)
        add_theta(mate_k, h)

    def add_mates(h):
        take(c_mate[h])
        add_theta(slot(1 - zl, dn), h)
        add_theta(slot(1 - zl, un), h)

    add_near(0)
    far_arrives(0)
    pl.when(is_same)(occupied_goes_on)

    @pl.when(is_cross)
    def _():
        occupied_part(0)

    add_theta(slot(zl, on), 0)
    add_near(1)
    add_mates(0)
    far_arrives(1)

    @pl.when(is_cross)
    def _():
        occupied_part(1)

    c_zfar[0].wait_recv()
    add_theta(slot(1 - zl, on), 0)

    def t_block(i, h):
        return ttbuf.at[i, :, lanes[h]]

    def t_flows(count, make):
        return [[make(w, h) for h in PARTS] for w in range(count)]

    t_z = t_flows(2, lambda w, h: flow(ttown.at[w, :, cols[h]], t_block(2 + w, h), zmate))
    t_xx = t_flows(2, lambda w, h: flow(ttown.at[w, :, cols[h]], t_block(w, h), xmate))
    t_sib = t_flows(2, lambda w, h: flow(t_block(w, h), t_block(w, h), sib))
    t_sibz = t_flows(2, lambda w, h: flow(t_block(2 + w, h), t_block(2 + w, h), sib))
    t_right = t_flows(2, lambda w, h: flow(t_block(w * (1 + same), h), t_block(4 + w, h), right))
    t_left = t_flows(2, lambda w, h: flow(t_block(same + w * (1 + same), h), t_block(6 + w, h), left))
    low_r = (x + 1) % 4 < 2
    low_l = (x + 3) % 4 < 2
    go_r = 4 + jnp.where(is_same & jnp.logical_not(low_r), 1, 0)
    go_l = 6 + jnp.where(is_same & low_l, 0, 1)
    t_far = [[flow(t_block(go_r, h), t_block(8, h), right) for h in PARTS],
             [flow(t_block(go_l, h), t_block(9, h), left) for h in PARTS]]
    t_relay = [[flow(t_block(i, h), t_block(i, h), sib) for h in PARTS] for i in range(4, 10)]

    def publish(h):
        for w in range(2):
            t = acc[pl.ds(w * ELEC, ELEC), cols[h]].astype(BF16)
            ttown[w, :, cols[h]] = t

            @pl.when(is_same)
            def _():
                ttbuf[w, :, lanes[h]] = t

            dens[pl.ds(w, 1), cols[h]] = jnp.sum(
                t.astype(F32) * otown[:, cols[h]].astype(F32), axis=0, keepdims=True)

        @pl.when(is_same)
        def _():
            start(t_right[0][h], t_left[0][h], t_sib[0][h], t_sib[1][h])

    publish(0)
    heard(3)

    @pl.when(is_cross)
    def _():
        start(t_xx[0][0], t_xx[1][0])

    add_theta(slot(zl, on), 1)
    add_near(2)
    far_arrives(2)
    start(t_z[0][0])

    @pl.when(is_cross)
    def _():
        start(t_z[1][0])

    @pl.when(is_cross)
    def _():
        occupied_part(2)

    add_mates(1)
    c_zfar[1].wait_recv()
    add_theta(slot(1 - zl, on), 1)
    publish(1)

    add_theta(slot(zl, on), 2)
    add_mates(2)
    c_zfar[2].wait_recv()
    add_theta(slot(1 - zl, on), 2)
    publish(2)

    dbuf[a] = dens[...].astype(BF16).astype(F32)

    def d_flow(r):
        return pltpu.make_async_remote_copy(
            src_ref=dbuf.at[a], dst_ref=dbuf.at[a], send_sem=d_send.at[r], recv_sem=d_recv.at[r],
            device_id={"pts": (a + r) % 16, "wlk": g}, device_id_type=MESH)

    def d_start(r, carry):
        d_flow(r).start()
        return carry

    def d_wait(r, carry):
        d_flow(r).wait()
        return carry

    lax.fori_loop(1, 16, d_start, 0)

    @pl.when(is_cross)
    def _():
        start(t_xx[0][1], t_xx[1][1], t_xx[0][2], t_xx[1][2], t_z[0][1], t_z[1][1], t_z[0][2], t_z[1][2])

    @pl.when(is_same)
    def _():
        start(t_z[0][1], t_z[0][2], *t_z[1])

    def turned(src, size):
        trans[pl.ds(0, ELEC), pl.ds(0, size)] = src.astype(F32)
        return jnp.swapaxes(trans[:, pl.ds(0, size)], 0, 1).astype(BF16)

    def turn(side, h):
        tp[side, cols[h], :] = turned(ttbuf[side, :, lanes[h]], CHUNK[h][1])

    def potential(first):
        if first == 0:
            pot[...] = jnp.zeros_like(pot)

        def add_chip(j, carry):
            one, two = dbuf[2 * j].astype(BF16), dbuf[2 * j + 1].astype(BF16)
            both = jnp.concatenate([v[:, i:i + n] for i, n in CHUNK for v in (one, two)], axis=1)
            pot[...] += lax.dot_general(both, kb[j], (((1,), (1,)), ((), ())), preferred_element_type=F32)
            return carry

        lax.fori_loop(first, first + 4, add_chip, 0)
        if first:
            pot_out[...] = pot[:, pl.ds(0, PTS)]

    exch[...] = jnp.zeros_like(exch)

    def unit(tt, side, ot, chip, weight, h):
        left_t = tp[side, pl.ds(0, ROWS), pl.ds(0, ELEC)]
        left_o = op[pl.ds(0, ROWS), pl.ds(0, ELEC)]

        def step(n, carry):
            part = pl.ds(n * 256, 256)
            near = dot(left_t, otbuf[ot, :, part])
            away = dot(left_o, ttbuf[tt, :, part])
            terms = kb[chip, :, part].astype(F32) * near * away
            return carry + terms.reshape(ROWS // 8, 8, 256).sum(axis=0)

        total = jnp.zeros((8, 256), F32)
        for n in range(*STEPS[h]):
            total = step(n, total)
        exch[side] += weight * total

    def cross_go(w, h):
        t_xx[w][h].wait_recv()
        start(t_right[w][h], t_left[w][h], t_sib[w][h])

    def z_take(w, h):
        t_z[w][h].wait_recv()
        turn(2 + w, h)

    def same_go(w, h):
        t_z[w][h].wait_recv()
        start(t_right[1][h] if w == 0 else t_left[1][h], t_sibz[w][h])
        turn(2 + w, h)

    def from_left(w, h):
        t_right[w][h].wait_recv()
        t_relay[w][h].start()

    def from_right(w, h):
        t_left[w][h].wait_recv()
        t_relay[2 + w][h].start()

    def from_both(w, h):
        from_left(w, h)
        from_right(w, h)

    def from_far(w, h):
        t_far[w][h].wait_recv()
        t_relay[4 + w][h].start()

    base = jnp.where(is_same, zh, 1 - zh) * 4
    of_same = {0: (0, 0, 0, 1.0), 1: (1, 0, 0, 1.0), 2: (2, 0, 0, 1.0), 3: (3, 0, 0, 1.0),
               4: (0, 1, 3, 2.0), 5: (2, 1, 3, 2.0), 6: (1, 2, 1, 2.0), 7: (3, 2, 1, 2.0),
               8: (2 * (x // 2), 3, 2, 2.0), 9: (2 * (x // 2) + 1, 3, 2, 2.0)}
    of_cross = {0: (2, 0, 0, 2.0), 1: (3, 0, 0, 2.0), 4: (2, 1, 3, 2.0), 5: (3, 1, 3, 2.0),
                6: (2, 2, 1, 2.0), 7: (3, 2, 1, 2.0), 8: (2, 3, 2, 2.0), 9: (3, 3, 2, 2.0)}

    def handed(i, h):
        return t_sib[i][h] if i < 2 else t_sibz[i - 2][h] if i < 4 else t_relay[i - 4][h]

    def run(s_block, x_block, h):
        @pl.when(is_same)
        def _():
            handed(s_block, h).wait_recv()

        @pl.when(is_cross)
        def _():
            handed(x_block, h).wait_recv()

        picked = [jnp.where(is_same, u, v) for u, v in zip((s_block, *of_same[s_block]), (x_block, *of_cross[x_block]))]
        unit(picked[0], picked[1], picked[2], base + (x + picked[3]) % 4, picked[4], h)

    def own(i, h):
        handed(i, h).wait_recv()
        side, ot, away, weight = of_same[i]
        unit(i, side, ot, base + (x + away) % 4, weight, h)

    op[...] = turned(otown[...], PAD)

    @pl.when(is_cross)
    def _():
        cross_go(0, 0)

    cut_kernel(2)

    @pl.when(is_same)
    def _():
        same_go(0, 0)
        from_both(0, 0)

    @pl.when(is_cross)
    def _():
        cross_go(1, 0)

    cut_kernel(3)
    kb[:, pl.ds(PTS, ROWS - PTS), :] = jnp.zeros((8, ROWS - PTS, 2 * PAD), BF16)
    take(o_sib)

    @pl.when(is_same)
    def _():
        for w in range(2):
            for h in PARTS:
                turn(w, h)
        own(0, 0)
        own(0, 1)
        own(0, 2)
        same_go(1, 0)
        own(1, 0)
        own(1, 1)
        own(1, 2)
        from_both(0, 1)

    @pl.when(is_cross)
    def _():
        z_take(0, 0)

    take(o_far)
    start(*o_relay[2])
    lax.fori_loop(1, 16, d_wait, 0)
    potential(0)

    @pl.when(is_cross)
    def _():
        from_both(0, 0)
        z_take(0, 1)
        cross_go(0, 1)

    @pl.when(is_same)
    def _():
        from_both(0, 2)
        same_go(0, 1)

    potential(4)
    for part in o_relay:
        take(part)

    @pl.when(is_cross)
    def _():
        z_take(0, 2)
        from_both(1, 0)

    run(4, 0, 0)

    @pl.when(is_cross)
    def _():
        cross_go(1, 1)
        t_far[0][0].start()
        t_far[1][0].start()

    run(4, 0, 1)

    @pl.when(is_same)
    def _():
        from_left(1, 0)
        t_far[0][0].start()
        same_go(1, 1)

    run(6, 4, 0)

    @pl.when(is_cross)
    def _():
        cross_go(0, 2)

    run(2, 6, 0)

    @pl.when(is_same)
    def _():
        same_go(0, 2)
        from_right(1, 0)
        t_far[1][0].start()

    @pl.when(is_cross)
    def _():
        z_take(1, 0)

    run(4, 0, 2)

    @pl.when(is_cross)
    def _():
        cross_go(1, 2)
        from_both(0, 1)
        t_far[0][1].start()

    run(6, 4, 1)

    @pl.when(is_same)
    def _():
        same_go(1, 2)

    run(2, 6, 1)

    @pl.when(is_same)
    def _():
        from_left(1, 1)
        t_far[0][1].start()

    @pl.when(is_cross)
    def _():
        z_take(1, 1)
        z_take(1, 2)

    run(3, 1, 0)
    run(3, 1, 1)

    @pl.when(is_cross)
    def _():
        from_both(1, 1)
        t_far[1][1].start()

    run(5, 5, 0)

    @pl.when(is_same)
    def _():
        from_right(1, 1)
        t_far[1][1].start()

    run(7, 7, 0)
    run(6, 1, 2)
    from_far(0, 0)

    @pl.when(is_cross)
    def _():
        from_both(0, 2)
        t_far[0][2].start()

    @pl.when(is_same)
    def _():
        from_left(1, 2)
        t_far[0][2].start()

    run(5, 5, 1)
    run(8, 8, 0)
    from_far(1, 0)

    @pl.when(is_cross)
    def _():
        from_both(1, 2)
        t_far[1][2].start()

    @pl.when(is_same)
    def _():
        from_right(1, 2)
        t_far[1][2].start()

    run(7, 7, 1)
    run(9, 9, 0)
    run(2, 4, 2)
    run(3, 6, 2)
    run(5, 5, 2)
    from_far(0, 1)
    run(7, 7, 2)
    from_far(1, 1)
    run(8, 8, 1)
    from_far(0, 2)
    run(9, 9, 1)
    from_far(1, 2)
    run(8, 8, 2)
    run(9, 9, 2)

    row = lax.broadcasted_iota(jnp.int32, (8, 128), 0)
    tile = jnp.zeros((8, 128), F32)
    for side in range(4):
        tile = jnp.where(row == (zl * 2 + side) % 4, -0.5 * jnp.sum(exch[side]), tile)
    for w in range(2):
        tile = jnp.where(row == 4 + zl * 2 + w,
                         0.5 * jnp.sum(dens[pl.ds(w, 1), pl.ds(0, PTS)] * pot[pl.ds(w, 1), pl.ds(0, PTS)]), tile)
    ebuf[plane] = tile

    def e_flow(r):
        return pltpu.make_async_remote_copy(
            src_ref=ebuf.at[plane], dst_ref=ebuf.at[plane], send_sem=e_send.at[r], recv_sem=e_recv.at[r],
            device_id=plane_dev(r), device_id_type=MESH)

    def e_wait(r, carry):
        e_flow(r).wait()
        return carry

    for r in (*range(16, 32), *range(15, 0, -1)):
        e_flow(r).start()

    for pairs in (c_own, c_mate, c_far, t_z, t_right, t_left, t_sib, t_far, t_relay, o_relay):
        for pair in pairs:
            for cp in pair:
                cp.wait_send()
    for cp in c_z + c_zfar + o_first + o_far:
        cp.wait_send()

    @pl.when(is_cross)
    def _():
        for cp in o_xx + t_xx[0] + t_xx[1]:
            cp.wait_send()

    @pl.when(is_same)
    def _():
        for cp in t_sibz[0] + t_sibz[1]:
            cp.wait_send()

    lax.fori_loop(1, 32, e_wait, 0)
    sum_out[...] = ebuf[...].sum(axis=0)


def finish(pot, total, pot_out, cou_out, exc_out):
    zl = lax.axis_index("wlk") // 4
    pot_out[...] = pot[...]
    row = lax.broadcasted_iota(jnp.int32, (8, 128), 0)
    for w in range(2):
        exc_out[w] = jnp.sum(jnp.where(row == zl * 2 + w, total[...], 0.0)) * (1.0 / 128)
        cou_out[w] = jnp.sum(jnp.where(row == 4 + zl * 2 + w, total[...], 0.0)) * (1.0 / 128)


def local(green_half, collocation, occupied, kernel):
    any_space = pl.BlockSpec(memory_space=pl.ANY)
    vmem = pltpu.VMEM
    in_vmem, in_smem = pl.BlockSpec(memory_space=vmem), pl.BlockSpec(memory_space=pltpu.SMEM)
    pot, total = pl.pallas_call(
        body,
        out_shape=(jax.ShapeDtypeStruct((2, PTS), F32), jax.ShapeDtypeStruct((8, 128), F32)),
        in_specs=[any_space] * 4,
        out_specs=(in_vmem, in_vmem),
        scratch_shapes=[
            vmem((DEEP, PTS), BF16),
            vmem((ELEC, PTS), BF16),
            vmem((2 * ELEC, 8 * DEEP), BF16),
            vmem((GROUPS, 2 * ELEC, 384), BF16),
            vmem((2, KCH, 16 * PTS), BF16),
            vmem((8, ROWS, 2 * PAD), BF16),
            vmem((GROUPS, DEEP_PAD, PAD), BF16),
            vmem((2 * ELEC, PAD), F32),
            vmem((2, ELEC, PAD), BF16),
            vmem((10, ELEC, 2 * PAD), BF16),
            vmem((4, PAD, 512), BF16),
            vmem((PAD, 512), BF16),
            vmem((ELEC, PAD), BF16),
            vmem((4, ELEC, 2 * PAD), BF16),
            vmem((512, PAD), F32),
            vmem((2, PAD), F32),
            vmem((16, 2, PAD), F32),
            vmem((32, 8, 128), F32),
            vmem((4, 8, 256), F32),
            vmem((2, ROWS), F32),
            pltpu.SemaphoreType.DMA((8,)),
            pltpu.SemaphoreType.DMA((FLOWS,)),
            pltpu.SemaphoreType.DMA((FLOWS,)),
            pltpu.SemaphoreType.DMA((16,)),
            pltpu.SemaphoreType.DMA((16,)),
            pltpu.SemaphoreType.DMA((32,)),
            pltpu.SemaphoreType.DMA((32,)),
            pltpu.SemaphoreType.REGULAR((4,)),
        ],
        compiler_params=pltpu.CompilerParams(
            collective_id=0, has_side_effects=True, vmem_limit_bytes=67_000_000),
    )(green_half, collocation, occupied.T, kernel)
    return pl.pallas_call(
        finish,
        out_shape=(jax.ShapeDtypeStruct((2, PTS), F32), jax.ShapeDtypeStruct((2,), F32), jax.ShapeDtypeStruct((2,), F32)),
        in_specs=[in_vmem, in_vmem],
        out_specs=(in_vmem, in_smem, in_smem),
    )(pot, total)


def solution(mesh):
    placed = (P("wlk", None, None), P("wlk", "pts"), P("pts", None), P("pts", None))
    return jax.shard_map(
        local,
        mesh=mesh,
        in_specs=placed,
        out_specs=(P("wlk", "pts"), P("wlk"), P("wlk")),
        check_vma=False,
    )
```

profile of v0, /device:TPU:1, one launch (start us, length us, event | category | flops | bytes accessed | tf_op | source)
XLA Modules:
  0.0 85.5 jit_solution(18215290404432686838)
XLA Ops:
  0.6 83.3 %shard_map.67 = (f32[2,600]{1,0:T(2,128)}, f32[8,128]{1,0:T(8,128)}) custom-call(bf16[2,400,2400]{2,1,0:T(8,128)(2,1)} %green.1, bf16[300,600]{1,0:T(8,128)(2,1)} %colloc.1, bf16[400,600]{1,0:T(8,128)(2,1)} %bitcast.1, bf16[600,9600]{1,0:T(8,128)(2,1)} %kmat.1), custom_call_target="tpu_custom_call" | custom-call | tf_op jit(solution)/shard_map/pallas_call | solution.py:692
  84.0 1.3 %shard_map.68 = (f32[2,600]{1,0:T(2,128)}, f32[2]{0:T(128)}, f32[2]{0:T(128)}) custom-call(f32[2,600]{1,0:T(2,128)} %get-tuple-element.5.pot, f32[8,128]{1,0:T(8,128)} %get-tuple-element.6.total), custom_call_target="tpu_custom_call" | custom-call | tf_op jit(solution)/shard_map/pallas_call | solution.py:730
where the time goes:
time: 85.6 us; the launch traced here: 85.5 us
  Pallas kernels  84.7 us (99%)
    pallas_call x1, Pallas kernels, local(): pl.pallas_call(body, out_shape=(jax.ShapeDtypeStruct((2, PTS), F32), jax....  83.3 us

commit v1 on v0

--- a/solution.py
+++ b/solution.py
@@ -114,16 +114,19 @@
 
     own_k, mate_k = slot(zl, y), slot(1 - zl, y)
     dn, un, on = (y + 3) % 4, (y + 1) % 4, (y + 2) % 4
-    c_z, c_own, c_mate, c_far, c_zfar = [], [], [], [], []
+    c_z, c_own, c_mate, c_far, c_zfar, c_matefar = [], [], [], [], [], []
     for h in PARTS:
         c_z.append(c_flow(own_k, h, zmate))
         c_own.append((c_flow(own_k, h, up), c_flow(own_k, h, down)))
         c_mate.append((c_flow(mate_k, h, up), c_flow(mate_k, h, down)))
         c_far.append((c_flow(slot(zl, dn), h, up, 0, C_CUT),
                       c_flow(slot(zl, un), h, down, C_CUT, DEEP_PAD - C_CUT)))
-        c_zfar.append(c_flow(slot(zl, on), h, zmate))
-    for h in PARTS:
-        start(*c_own[h], c_z[h])
+        if h == 0:
+            c_zfar.append(c_flow(slot(zl, on), h, zmate))
+        else:
+            c_matefar.append((c_flow(slot(1 - zl, dn), h, up, 0, C_CUT),
+                              c_flow(slot(1 - zl, un), h, down, C_CUT, DEEP_PAD - C_CUT)))
+    start(*c_own[0], c_z[0], *c_own[1], c_z[1], c_z[2])
 
     def o_block(i, h):
         return otbuf.at[i, :, lanes[h]]
@@ -202,38 +205,19 @@
 
     def far_arrives(h):
         take(c_far[h])
-        c_zfar[h].start()
+        if h == 0:
+            c_zfar[0].start()
 
     for h in PARTS:
         add_theta(own_k, h, True)
-    cut_kernel(0)
-    heard(1)
-    near_arrives(0)
-
-    @pl.when(is_cross)
-    def _():
-        o_xx[0].wait_recv()
-        start(o_right[0], o_left[0], o_sib[0])
-
-    cut_kernel(1)
-    near_arrives(1)
-    near_arrives(2)
-    heard(2)
-
-    @pl.when(is_cross)
-    def _():
-        for h in (1, 2):
-            o_xx[h].wait_recv()
-            start(o_right[h], o_left[h], o_sib[h])
-
     def occupied_part(h):
         o_right[h].wait_recv()
         o_left[h].wait_recv()
         start(o_far[h], o_relay[0][h], o_relay[1][h])
 
-    def occupied_goes_on():
-        for h in PARTS:
-            occupied_part(h)
+    def occupied_from_z(h):
+        o_xx[h].wait_recv()
+        start(o_right[h], o_left[h], o_sib[h])
 
     def add_near(h):
         add_theta(slot(zl, dn), h)
@@ -242,26 +226,49 @@
 
     def add_mates(h):
         take(c_mate[h])
+        if h:
+            start(*c_matefar[h - 1])
         add_theta(slot(1 - zl, dn), h)
         add_theta(slot(1 - zl, un), h)
 
+    cut_kernel(0)
+    heard(1)
+    near_arrives(0)
+    start(*c_own[2])
+
+    @pl.when(is_cross)
+    def _():
+        occupied_from_z(0)
+
     add_near(0)
+    cut_kernel(1)
+    near_arrives(1)
+
+    @pl.when(is_cross)
+    def _():
+        occupied_from_z(1)
+
     far_arrives(0)
-    pl.when(is_same)(occupied_goes_on)
-
-    @pl.when(is_cross)
+
+    @pl.when(is_same)
     def _():
         occupied_part(0)
 
     add_theta(slot(zl, on), 0)
+    heard(2)
     add_near(1)
+
+    @pl.when(is_cross)
+    def _():
+        occupied_from_z(2)
+
+    @pl.when(is_same)
+    def _():
+        occupied_part(1)
+        occupied_part(2)
+
+    cut_kernel(3)
     add_mates(0)
-    far_arrives(1)
-
-    @pl.when(is_cross)
-    def _():
-        occupied_part(1)
-
     c_zfar[0].wait_recv()
     add_theta(slot(1 - zl, on), 0)
 
@@ -285,6 +292,35 @@
              [flow(t_block(go_l, h), t_block(9, h), left) for h in PARTS]]
     t_relay = [[flow(t_block(i, h), t_block(i, h), sib) for h in PARTS] for i in range(4, 10)]
 
+    def turned(src, size):
+        trans[pl.ds(0, ELEC), pl.ds(0, size)] = src.astype(F32)
+        return jnp.swapaxes(trans[:, pl.ds(0, size)], 0, 1).astype(BF16)
+
+    def turn(side, h):
+        tp[side, cols[h], :] = turned(ttbuf[side, :, lanes[h]], CHUNK[h][1])
+
+    def cross_go(w, h):
+        t_xx[w][h].wait_recv()
+        start(t_right[w][h], t_left[w][h], t_sib[w][h])
+
+    def same_go(w, h):
+        t_z[w][h].wait_recv()
+        start(t_right[1][h] if w == 0 else t_left[1][h], t_sibz[w][h])
+        turn(2 + w, h)
+
+    def d_flow(r):
+        return pltpu.make_async_remote_copy(
+            src_ref=dbuf.at[a], dst_ref=dbuf.at[a], send_sem=d_send.at[r], recv_sem=d_recv.at[r],
+            device_id={"pts": (a + r) % 16, "wlk": g}, device_id_type=MESH)
+
+    def d_start(r, carry):
+        d_flow(r).start()
+        return carry
+
+    def d_wait(r, carry):
+        d_flow(r).wait()
+        return carry
+
     def publish(h):
         for w in range(2):
             t = acc[pl.ds(w * ELEC, ELEC), cols[h]].astype(BF16)
@@ -297,72 +333,67 @@
             dens[pl.ds(w, 1), cols[h]] = jnp.sum(
                 t.astype(F32) * otown[:, cols[h]].astype(F32), axis=0, keepdims=True)
 
+        if h == 2:
+            dbuf[a] = dens[...].astype(BF16).astype(F32)
+            lax.fori_loop(1, 16, d_start, 0)
+
         @pl.when(is_same)
         def _():
-            start(t_right[0][h], t_left[0][h], t_sib[0][h], t_sib[1][h])
+            start(t_right[0][h], t_left[0][h], t_z[0][h], t_sib[0][h], t_sib[1][h])
+            if h == 2:
+                start(*t_z[1])
+
+        @pl.when(is_cross)
+        def _():
+            if h == 1:
+                start(t_xx[0][1], t_z[0][1])
+            elif h == 0:
+                start(t_xx[0][0], t_z[0][0], t_xx[1][0], t_z[1][0])
+            else:
+                start(t_xx[1][1], t_z[1][1], t_xx[0][2], t_z[0][2], t_xx[1][2], t_z[1][2])
 
     publish(0)
     heard(3)
 
-    @pl.when(is_cross)
-    def _():
-        start(t_xx[0][0], t_xx[1][0])
+    near_arrives(2)
+    far_arrives(1)
+
+    @pl.when(is_cross)
+    def _():
+        occupied_part(0)
+
+    @pl.when(is_cross)
+    def _():
+        occupied_part(1)
 
     add_theta(slot(zl, on), 1)
+    cut_kernel(2)
+    add_mates(1)
+    far_arrives(2)
+
+    @pl.when(is_cross)
+    def _():
+        occupied_part(2)
+
     add_near(2)
-    far_arrives(2)
-    start(t_z[0][0])
-
-    @pl.when(is_cross)
-    def _():
-        start(t_z[1][0])
-
-    @pl.when(is_cross)
-    def _():
-        occupied_part(2)
-
-    add_mates(1)
-    c_zfar[1].wait_recv()
+    add_theta(slot(zl, on), 2)
+
+    @pl.when(is_cross)
+    def _():
+        cross_go(0, 0)
+
+    add_mates(2)
+    take(c_matefar[0])
     add_theta(slot(1 - zl, on), 1)
     publish(1)
 
-    add_theta(slot(zl, on), 2)
-    add_mates(2)
-    c_zfar[2].wait_recv()
+    take(c_matefar[1])
     add_theta(slot(1 - zl, on), 2)
     publish(2)
 
-    dbuf[a] = dens[...].astype(BF16).astype(F32)
-
-    def d_flow(r):
-        return pltpu.make_async_remote_copy(
-            src_ref=dbuf.at[a], dst_ref=dbuf.at[a], send_sem=d_send.at[r], recv_sem=d_recv.at[r],
-            device_id={"pts": (a + r) % 16, "wlk": g}, device_id_type=MESH)
-
-    def d_start(r, carry):
-        d_flow(r).start()
-        return carry
-
-    def d_wait(r, carry):
-        d_flow(r).wait()
-        return carry
-
-    lax.fori_loop(1, 16, d_start, 0)
-
-    @pl.when(is_cross)
-    def _():
-        start(t_xx[0][1], t_xx[1][1], t_xx[0][2], t_xx[1][2], t_z[0][1], t_z[1][1], t_z[0][2], t_z[1][2])
-
-    @pl.when(is_same)
-    def _():
-        start(t_z[0][1], t_z[0][2], *t_z[1])
-
-    def turned(src, size):
-        trans[pl.ds(0, ELEC), pl.ds(0, size)] = src.astype(F32)
-        return jnp.swapaxes(trans[:, pl.ds(0, size)], 0, 1).astype(BF16)
-
-    def turn(side, h):
-        tp[side, cols[h], :] = turned(ttbuf[side, :, lanes[h]], CHUNK[h][1])
+    @pl.when(is_same)
+    def _():
+        same_go(0, 0)
 
     def potential(first):
         if first == 0:
@@ -396,17 +427,8 @@
             total = step(n, total)
         exch[side] += weight * total
 
-    def cross_go(w, h):
-        t_xx[w][h].wait_recv()
-        start(t_right[w][h], t_left[w][h], t_sib[w][h])
-
     def z_take(w, h):
         t_z[w][h].wait_recv()
-        turn(2 + w, h)
-
-    def same_go(w, h):
-        t_z[w][h].wait_recv()
-        start(t_right[1][h] if w == 0 else t_left[1][h], t_sibz[w][h])
         turn(2 + w, h)
 
     def from_left(w, h):
@@ -456,20 +478,13 @@
 
     @pl.when(is_cross)
     def _():
-        cross_go(0, 0)
-
-    cut_kernel(2)
-
-    @pl.when(is_same)
-    def _():
-        same_go(0, 0)
+        cross_go(1, 0)
+
+    @pl.when(is_same)
+    def _():
+        same_go(1, 0)
         from_both(0, 0)
 
-    @pl.when(is_cross)
-    def _():
-        cross_go(1, 0)
-
-    cut_kernel(3)
     kb[:, pl.ds(PTS, ROWS - PTS), :] = jnp.zeros((8, ROWS - PTS, 2 * PAD), BF16)
     take(o_sib)
 
@@ -481,99 +496,94 @@
         own(0, 0)
         own(0, 1)
         own(0, 2)
-        same_go(1, 0)
+        same_go(0, 1)
+        from_both(0, 1)
         own(1, 0)
         own(1, 1)
         own(1, 2)
-        from_both(0, 1)
 
     @pl.when(is_cross)
     def _():
         z_take(0, 0)
+        from_both(0, 0)
+        cross_go(0, 1)
+        z_take(0, 1)
 
     take(o_far)
     start(*o_relay[2])
     lax.fori_loop(1, 16, d_wait, 0)
     potential(0)
 
-    @pl.when(is_cross)
-    def _():
-        from_both(0, 0)
-        z_take(0, 1)
-        cross_go(0, 1)
-
-    @pl.when(is_same)
-    def _():
-        from_both(0, 2)
-        same_go(0, 1)
+    @pl.when(is_same)
+    def _():
+        same_go(1, 1)
+        from_left(1, 0)
+        t_far[0][0].start()
+
+    @pl.when(is_cross)
+    def _():
+        from_both(1, 0)
+        cross_go(1, 1)
+        start(t_far[0][0], t_far[1][0])
+        z_take(0, 2)
 
     potential(4)
     for part in o_relay:
         take(part)
-
-    @pl.when(is_cross)
-    def _():
-        z_take(0, 2)
-        from_both(1, 0)
-
     run(4, 0, 0)
-
-    @pl.when(is_cross)
-    def _():
-        cross_go(1, 1)
-        t_far[0][0].start()
-        t_far[1][0].start()
-
     run(4, 0, 1)
 
     @pl.when(is_same)
     def _():
-        from_left(1, 0)
-        t_far[0][0].start()
-        same_go(1, 1)
-
-    run(6, 4, 0)
-
-    @pl.when(is_cross)
-    def _():
-        cross_go(0, 2)
-
-    run(2, 6, 0)
-
-    @pl.when(is_same)
-    def _():
         same_go(0, 2)
+        from_both(0, 2)
         from_right(1, 0)
         t_far[1][0].start()
 
     @pl.when(is_cross)
     def _():
-        z_take(1, 0)
-
-    run(4, 0, 2)
+        cross_go(0, 2)
+
+    run(6, 4, 0)
 
     @pl.when(is_cross)
     def _():
         cross_go(1, 2)
+
+    run(2, 6, 0)
+
+    @pl.when(is_same)
+    def _():
+        same_go(1, 2)
+
+    @pl.when(is_cross)
+    def _():
         from_both(0, 1)
         t_far[0][1].start()
 
-    run(6, 4, 1)
-
-    @pl.when(is_same)
-    def _():
-        same_go(1, 2)
-
-    run(2, 6, 1)
+    run(4, 0, 2)
 
     @pl.when(is_same)
     def _():
         from_left(1, 1)
         t_far[0][1].start()
 
-    @pl.when(is_cross)
-    def _():
+    run(6, 4, 1)
+
+    @pl.when(is_cross)
+    def _():
+        z_take(1, 0)
         z_take(1, 1)
+
+    run(2, 6, 1)
+
+    @pl.when(is_same)
+    def _():
+        from_right(1, 1)
+        t_far[1][1].start()
+
+    @pl.when(is_cross)
+    def _():
         z_take(1, 2)
 
     run(3, 1, 0)
@@ -585,13 +595,13 @@
         t_far[1][1].start()
 
     run(5, 5, 0)
-
-    @pl.when(is_same)
-    def _():
-        from_right(1, 1)
-        t_far[1][1].start()
-
     run(7, 7, 0)
+
+    @pl.when(is_same)
+    def _():
+        from_left(1, 2)
+        t_far[0][2].start()
+
     run(6, 1, 2)
     from_far(0, 0)
 
@@ -602,8 +612,8 @@
 
     @pl.when(is_same)
     def _():
-        from_left(1, 2)
-        t_far[0][2].start()
+        from_right(1, 2)
+        t_far[1][2].start()
 
     run(5, 5, 1)
     run(8, 8, 0)
@@ -612,11 +622,6 @@
     @pl.when(is_cross)
     def _():
         from_both(1, 2)
-        t_far[1][2].start()
-
-    @pl.when(is_same)
-    def _():
-        from_right(1, 2)
         t_far[1][2].start()
 
     run(7, 7, 1)
@@ -655,7 +660,7 @@
     for r in (*range(16, 32), *range(15, 0, -1)):
         e_flow(r).start()
 
-    for pairs in (c_own, c_mate, c_far, t_z, t_right, t_left, t_sib, t_far, t_relay, o_relay):
+    for pairs in (c_own, c_mate, c_far, c_matefar, t_z, t_right, t_left, t_sib, t_far, t_relay, o_relay):
         for pair in pairs:
             for cp in pair:
                 cp.wait_send()

time: 85.6 us -> 81.5 us (0.952)
  Pallas kernels: 84.7 us -> 80.5 us
    pallas_call x1, Pallas kernels: 83.3 us -> 79.2 us  [local(): pl.pallas_call(body, out_shape=(jax.ShapeDtypeStruct((2, PTS), F32), jax....]
where the time goes in v1:
time: 81.5 us; the launch traced here: 81.3 us
  Pallas kernels  80.5 us (99%)
    pallas_call x1, Pallas kernels, local(): pl.pallas_call(body, out_shape=(jax.ShapeDtypeStruct((2, PTS), F32), jax....  79.2 us

profile of v1, /device:TPU:1, one launch (start us, length us, event | category | flops | bytes accessed | tf_op | source)
XLA Modules:
  0.0 81.3 jit_solution(840440995831296347)
XLA Ops:
  0.6 79.2 %shard_map.67 = (f32[2,600]{1,0:T(2,128)}, f32[8,128]{1,0:T(8,128)}) custom-call(bf16[2,400,2400]{2,1,0:T(8,128)(2,1)} %green.1, bf16[300,600]{1,0:T(8,128)(2,1)} %colloc.1, bf16[400,600]{1,0:T(8,128)(2,1)} %bitcast.1, bf16[600,9600]{1,0:T(8,128)(2,1)} %kmat.1), custom_call_target="tpu_custom_call" | custom-call | tf_op jit(solution)/shard_map/pallas_call | solution.py:697
  79.8 1.3 %shard_map.68 = (f32[2,600]{1,0:T(2,128)}, f32[2]{0:T(128)}, f32[2]{0:T(128)}) custom-call(f32[2,600]{1,0:T(2,128)} %get-tuple-element.5.pot, f32[8,128]{1,0:T(8,128)} %get-tuple-element.6.total), custom_call_target="tpu_custom_call" | custom-call | tf_op jit(solution)/shard_map/pallas_call | solution.py:735

commit v2 on v1

--- a/solution.py
+++ b/solution.py
@@ -20,7 +20,7 @@
 CHUNK = ((0, 256), (256, 256), (512, 128))
 PARTS = range(len(CHUNK))
 STEPS = ((0, 2), (2, 4), (4, 5))
-FLOWS = 144
+FLOWS = 110
 
 
 def dot(a, b):
@@ -29,7 +29,7 @@
 
 def body(green, colloc, occ, kmat, pot_out, sum_out,
          cin, oin, gv, g8, kst, kb, cbuf, acc, ttown, ttbuf, tp, op, otown, otbuf,
-         trans, dens, dbuf, ebuf, exch, pot, local_sem, send, recv, d_send, d_recv, e_send, e_recv, hear):
+         trans, dens, dbuf, ebuf, exch, pot, local_sem, send, recv, d_sem, e_sem, hear, pot_all):
     a, g = lax.axis_index("pts"), lax.axis_index("wlk")
     zh, x, c = a // 8, (a // 2) % 4, a % 2
     zl, y = g // 4, g % 4
@@ -50,11 +50,15 @@
     cols = tuple(pl.ds(start, size) for start, size in CHUNK)
     numbers = iter(range(FLOWS))
 
-    def flow(src, dst, dev):
-        f = next(numbers)
+    def flow(src, dst, dev, group):
         return pltpu.make_async_remote_copy(
-            src_ref=src, dst_ref=dst, send_sem=send.at[f], recv_sem=recv.at[f],
+            src_ref=src, dst_ref=dst, send_sem=send.at[group], recv_sem=recv.at[next(numbers)],
             device_id=dev, device_id_type=MESH)
+
+    def sent(group, ref):
+        pltpu.make_async_remote_copy(
+            src_ref=ref, dst_ref=ref, send_sem=send.at[group], recv_sem=recv.at[0],
+            device_id=sib, device_id_type=MESH).wait_send()
 
     def start(*copies):
         for cp in copies:
@@ -108,36 +112,36 @@
     def slot(zlo, yy):
         return zlo * 4 + yy
 
-    def c_flow(k, h, dev, first=0, count=DEEP_PAD):
+    def c_flow(group, k, h, dev, first=0, count=DEEP_PAD):
         ref = cbuf.at[k, pl.ds(first, count), cols[h]]
-        return flow(ref, ref, dev)
+        return flow(ref, ref, dev, group)
 
     own_k, mate_k = slot(zl, y), slot(1 - zl, y)
     dn, un, on = (y + 3) % 4, (y + 1) % 4, (y + 2) % 4
     c_z, c_own, c_mate, c_far, c_zfar, c_matefar = [], [], [], [], [], []
     for h in PARTS:
-        c_z.append(c_flow(own_k, h, zmate))
-        c_own.append((c_flow(own_k, h, up), c_flow(own_k, h, down)))
-        c_mate.append((c_flow(mate_k, h, up), c_flow(mate_k, h, down)))
-        c_far.append((c_flow(slot(zl, dn), h, up, 0, C_CUT),
-                      c_flow(slot(zl, un), h, down, C_CUT, DEEP_PAD - C_CUT)))
+        c_z.append(c_flow(0, own_k, h, zmate))
+        c_own.append((c_flow(1, own_k, h, up), c_flow(1, own_k, h, down)))
+        c_mate.append((c_flow(2, mate_k, h, up), c_flow(2, mate_k, h, down)))
+        c_far.append((c_flow(3, slot(zl, dn), h, up, 0, C_CUT),
+                      c_flow(3, slot(zl, un), h, down, C_CUT, DEEP_PAD - C_CUT)))
         if h == 0:
-            c_zfar.append(c_flow(slot(zl, on), h, zmate))
+            c_zfar.append(c_flow(4, slot(zl, on), h, zmate))
         else:
-            c_matefar.append((c_flow(slot(1 - zl, dn), h, up, 0, C_CUT),
-                              c_flow(slot(1 - zl, un), h, down, C_CUT, DEEP_PAD - C_CUT)))
+            c_matefar.append((c_flow(5, slot(1 - zl, dn), h, up, 0, C_CUT),
+                              c_flow(5, slot(1 - zl, un), h, down, C_CUT, DEEP_PAD - C_CUT)))
     start(*c_own[0], c_z[0], *c_own[1], c_z[1], c_z[2])
 
     def o_block(i, h):
         return otbuf.at[i, :, lanes[h]]
 
-    o_xx = [flow(otown.at[:, cols[h]], o_block(0, h), xmate) for h in PARTS]
-    o_right = [flow(o_block(0, h), o_block(1, h), right) for h in PARTS]
-    o_left = [flow(o_block(0, h), o_block(2, h), left) for h in PARTS]
-    o_sib = [flow(o_block(0, h), o_block(0, h), sib) for h in PARTS]
-    o_far = [flow(o_block(1, 0), o_block(3, 0), right), flow(o_block(2, 1), o_block(3, 1), left),
-             flow(o_block(1, 2), o_block(3, 2), right)]
-    o_relay = [[flow(o_block(i, h), o_block(i, h), sib) for h in PARTS] for i in (1, 2, 3)]
+    o_xx = [flow(otown.at[:, cols[h]], o_block(0, h), xmate, 6) for h in PARTS]
+    o_right = [flow(o_block(0, h), o_block(1, h), right, 7) for h in PARTS]
+    o_left = [flow(o_block(0, h), o_block(2, h), left, 8) for h in PARTS]
+    o_sib = [flow(o_block(0, h), o_block(0, h), sib, 9) for h in PARTS]
+    o_far = [flow(o_block(1, 0), o_block(3, 0), right, 10), flow(o_block(2, 1), o_block(3, 1), left, 10),
+             flow(o_block(1, 2), o_block(3, 2), right, 10)]
+    o_relay = [[flow(o_block(i, h), o_block(i, h), sib, 11 + i // 3) for h in PARTS] for i in (1, 2, 3)]
     o_first = o_right + o_left + o_sib
 
     @pl.when(is_cross)
@@ -278,19 +282,19 @@
     def t_flows(count, make):
         return [[make(w, h) for h in PARTS] for w in range(count)]
 
-    t_z = t_flows(2, lambda w, h: flow(ttown.at[w, :, cols[h]], t_block(2 + w, h), zmate))
-    t_xx = t_flows(2, lambda w, h: flow(ttown.at[w, :, cols[h]], t_block(w, h), xmate))
-    t_sib = t_flows(2, lambda w, h: flow(t_block(w, h), t_block(w, h), sib))
-    t_sibz = t_flows(2, lambda w, h: flow(t_block(2 + w, h), t_block(2 + w, h), sib))
-    t_right = t_flows(2, lambda w, h: flow(t_block(w * (1 + same), h), t_block(4 + w, h), right))
-    t_left = t_flows(2, lambda w, h: flow(t_block(same + w * (1 + same), h), t_block(6 + w, h), left))
+    t_z = t_flows(2, lambda w, h: flow(ttown.at[w, :, cols[h]], t_block(2 + w, h), zmate, 13))
+    t_xx = t_flows(2, lambda w, h: flow(ttown.at[w, :, cols[h]], t_block(w, h), xmate, 14))
+    t_sib = t_flows(2, lambda w, h: flow(t_block(w, h), t_block(w, h), sib, 15))
+    t_sibz = t_flows(2, lambda w, h: flow(t_block(2 + w, h), t_block(2 + w, h), sib, 16))
+    t_right = t_flows(2, lambda w, h: flow(t_block(w * (1 + same), h), t_block(4 + w, h), right, 17))
+    t_left = t_flows(2, lambda w, h: flow(t_block(same + w * (1 + same), h), t_block(6 + w, h), left, 18))
     low_r = (x + 1) % 4 < 2
     low_l = (x + 3) % 4 < 2
     go_r = 4 + jnp.where(is_same & jnp.logical_not(low_r), 1, 0)
     go_l = 6 + jnp.where(is_same & low_l, 0, 1)
-    t_far = [[flow(t_block(go_r, h), t_block(8, h), right) for h in PARTS],
-             [flow(t_block(go_l, h), t_block(9, h), left) for h in PARTS]]
-    t_relay = [[flow(t_block(i, h), t_block(i, h), sib) for h in PARTS] for i in range(4, 10)]
+    t_far = [[flow(t_block(go_r, h), t_block(8, h), right, 19) for h in PARTS],
+             [flow(t_block(go_l, h), t_block(9, h), left, 19) for h in PARTS]]
+    t_relay = [[flow(t_block(i, h), t_block(i, h), sib, 20) for h in PARTS] for i in range(4, 10)]
 
     def turned(src, size):
         trans[pl.ds(0, ELEC), pl.ds(0, size)] = src.astype(F32)
@@ -310,16 +314,18 @@
 
     def d_flow(r):
         return pltpu.make_async_remote_copy(
-            src_ref=dbuf.at[a], dst_ref=dbuf.at[a], send_sem=d_send.at[r], recv_sem=d_recv.at[r],
+            src_ref=dbuf.at[a], dst_ref=dbuf.at[a], send_sem=d_sem.at[0], recv_sem=d_sem.at[1],
             device_id={"pts": (a + r) % 16, "wlk": g}, device_id_type=MESH)
 
     def d_start(r, carry):
         d_flow(r).start()
         return carry
 
-    def d_wait(r, carry):
-        d_flow(r).wait()
-        return carry
+    def d_wait():
+        every = dbuf.at[pl.ds(0, 15)]
+        pltpu.make_async_remote_copy(
+            src_ref=every, dst_ref=every, send_sem=d_sem.at[0], recv_sem=d_sem.at[1],
+            device_id=sib, device_id_type=MESH).wait()
 
     def publish(h):
         for w in range(2):
@@ -407,8 +413,10 @@
 
         lax.fori_loop(first, first + 4, add_chip, 0)
         if first:
-            pot_out[...] = pot[:, pl.ds(0, PTS)]
-
+            pot_all[...] = pot[:, pl.ds(0, PTS)]
+            save_pot.start()
+
+    save_pot = pltpu.make_async_copy(pot_all, pot_out, local_sem.at[0])
     exch[...] = jnp.zeros_like(exch)
 
     def unit(tt, side, ot, chip, weight, h):
@@ -496,11 +504,11 @@
         own(0, 0)
         own(0, 1)
         own(0, 2)
+        own(1, 0)
         same_go(0, 1)
-        from_both(0, 1)
-        own(1, 0)
         own(1, 1)
         own(1, 2)
+        from_both(0, 1)
 
     @pl.when(is_cross)
     def _():
@@ -511,14 +519,12 @@
 
     take(o_far)
     start(*o_relay[2])
-    lax.fori_loop(1, 16, d_wait, 0)
+    d_wait()
     potential(0)
 
     @pl.when(is_same)
     def _():
         same_go(1, 1)
-        from_left(1, 0)
-        t_far[0][0].start()
 
     @pl.when(is_cross)
     def _():
@@ -535,6 +541,8 @@
 
     @pl.when(is_same)
     def _():
+        from_left(1, 0)
+        t_far[0][0].start()
         same_go(0, 2)
         from_both(0, 2)
         from_right(1, 0)
@@ -650,34 +658,33 @@
 
     def e_flow(r):
         return pltpu.make_async_remote_copy(
-            src_ref=ebuf.at[plane], dst_ref=ebuf.at[plane], send_sem=e_send.at[r], recv_sem=e_recv.at[r],
+            src_ref=ebuf.at[plane], dst_ref=ebuf.at[plane], send_sem=e_sem.at[0], recv_sem=e_sem.at[1],
             device_id=plane_dev(r), device_id_type=MESH)
-
-    def e_wait(r, carry):
-        e_flow(r).wait()
-        return carry
 
     for r in (*range(16, 32), *range(15, 0, -1)):
         e_flow(r).start()
 
-    for pairs in (c_own, c_mate, c_far, c_matefar, t_z, t_right, t_left, t_sib, t_far, t_relay, o_relay):
-        for pair in pairs:
-            for cp in pair:
-                cp.wait_send()
-    for cp in c_z + c_zfar + o_first + o_far:
-        cp.wait_send()
-
-    @pl.when(is_cross)
-    def _():
-        for cp in o_xx + t_xx[0] + t_xx[1]:
-            cp.wait_send()
-
-    @pl.when(is_same)
-    def _():
-        for cp in t_sibz[0] + t_sibz[1]:
-            cp.wait_send()
-
-    lax.fori_loop(1, 32, e_wait, 0)
+    for group, ref in ((0, cbuf.at[0]), (1, cbuf.at[pl.ds(0, 2)]), (2, cbuf.at[pl.ds(0, 2)]), (3, cbuf.at[0]),
+                       (4, cbuf.at[0, :, cols[0]]), (5, cbuf.at[0, :, pl.ds(256, 384)]),
+                       (7, otown), (8, otown), (9, otown), (10, otown), (11, otbuf.at[0]), (12, otown),
+                       (13, ttown), (15, ttown), (17, ttown), (18, ttown), (19, ttown), (20, ttbuf.at[pl.ds(0, 3)])):
+        sent(group, ref)
+
+    @pl.when(is_cross)
+    def _():
+        sent(6, otown)
+        sent(14, ttown)
+
+    @pl.when(is_same)
+    def _():
+        sent(16, ttown)
+
+    save_pot.wait()
+    every = ebuf.at[pl.ds(0, 31)]
+    last = pltpu.make_async_remote_copy(
+        src_ref=every, dst_ref=every, send_sem=e_sem.at[0], recv_sem=e_sem.at[1],
+        device_id=sib, device_id_type=MESH)
+    last.wait()
     sum_out[...] = ebuf[...].sum(axis=0)
 
 
@@ -698,7 +705,7 @@
         body,
         out_shape=(jax.ShapeDtypeStruct((2, PTS), F32), jax.ShapeDtypeStruct((8, 128), F32)),
         in_specs=[any_space] * 4,
-        out_specs=(in_vmem, in_vmem),
+        out_specs=(any_space, in_vmem),
         scratch_shapes=[
             vmem((DEEP, PTS), BF16),
             vmem((ELEC, PTS), BF16),
@@ -721,13 +728,12 @@
             vmem((4, 8, 256), F32),
             vmem((2, ROWS), F32),
             pltpu.SemaphoreType.DMA((8,)),
+            pltpu.SemaphoreType.DMA((21,)),
             pltpu.SemaphoreType.DMA((FLOWS,)),
-            pltpu.SemaphoreType.DMA((FLOWS,)),
-            pltpu.SemaphoreType.DMA((16,)),
-            pltpu.SemaphoreType.DMA((16,)),
-            pltpu.SemaphoreType.DMA((32,)),
-            pltpu.SemaphoreType.DMA((32,)),
+            pltpu.SemaphoreType.DMA((2,)),
+            pltpu.SemaphoreType.DMA((2,)),
             pltpu.SemaphoreType.REGULAR((4,)),
+            vmem((2, PTS), F32),
         ],
         compiler_params=pltpu.CompilerParams(
             collective_id=0, has_side_effects=True, vmem_limit_bytes=67_000_000),

time: 81.5 us -> 78.9 us (0.968)
  Pallas kernels: 80.5 us -> 77.9 us
    pallas_call x1, Pallas kernels: 79.2 us -> 76.6 us  [local(): pl.pallas_call(body, out_shape=(jax.ShapeDtypeStruct((2, PTS), F32), jax....]
where the time goes in v2:
time: 78.9 us; the launch traced here: 78.7 us
  Pallas kernels  77.9 us (99%)
  between operations  0.8 us (1%)
    pallas_call x1, Pallas kernels, local(): pl.pallas_call(body, out_shape=(jax.ShapeDtypeStruct((2, PTS), F32), jax....  76.6 us

profile of v2, /device:TPU:1, one launch (start us, length us, event | category | flops | bytes accessed | tf_op | source)
XLA Modules:
  0.0 78.7 jit_solution(5371655026262129967)
XLA Ops:
  0.6 76.6 %shard_map.67 = (f32[2,600]{1,0:T(2,128)}, f32[8,128]{1,0:T(8,128)}) custom-call(bf16[2,400,2400]{2,1,0:T(8,128)(2,1)} %green.1, bf16[300,600]{1,0:T(8,128)(2,1)} %colloc.1, bf16[400,600]{1,0:T(8,128)(2,1)} %bitcast.1, bf16[600,9600]{1,0:T(8,128)(2,1)} %kmat.1), custom_call_target="tpu_custom_call" | custom-call | tf_op jit(solution)/shard_map/pallas_call | solution.py:704
  77.2 1.3 %shard_map.68 = (f32[2,600]{1,0:T(2,128)}, f32[2]{0:T(128)}, f32[2]{0:T(128)}) custom-call(f32[2,600]{1,0:T(2,128)} %get-tuple-element.5.pot, f32[8,128]{1,0:T(8,128)} %get-tuple-element.6.total), custom_call_target="tpu_custom_call" | custom-call | tf_op jit(solution)/shard_map/pallas_call | solution.py:741

commit v3 on v2

--- a/solution.py
+++ b/solution.py
@@ -605,25 +605,26 @@
     run(5, 5, 0)
     run(7, 7, 0)
 
+    run(6, 1, 2)
+    from_far(0, 0)
+
+    @pl.when(is_cross)
+    def _():
+        from_both(0, 2)
+        t_far[0][2].start()
+
+    @pl.when(is_same)
+    def _():
+        from_right(1, 2)
+        t_far[1][2].start()
+
+    run(5, 5, 1)
+
     @pl.when(is_same)
     def _():
         from_left(1, 2)
         t_far[0][2].start()
 
-    run(6, 1, 2)
-    from_far(0, 0)
-
-    @pl.when(is_cross)
-    def _():
-        from_both(0, 2)
-        t_far[0][2].start()
-
-    @pl.when(is_same)
-    def _():
-        from_right(1, 2)
-        t_far[1][2].start()
-
-    run(5, 5, 1)
     run(8, 8, 0)
     from_far(1, 0)
 
@@ -647,12 +648,12 @@
     run(8, 8, 2)
     run(9, 9, 2)
 
-    row = lax.broadcasted_iota(jnp.int32, (8, 128), 0)
-    tile = jnp.zeros((8, 128), F32)
+    lane = lax.broadcasted_iota(jnp.int32, (1, 128), 1)
+    tile = jnp.zeros((1, 128), F32)
     for side in range(4):
-        tile = jnp.where(row == (zl * 2 + side) % 4, -0.5 * jnp.sum(exch[side]), tile)
+        tile = jnp.where(lane == (zl * 2 + side) % 4, -0.5 * jnp.sum(exch[side]), tile)
     for w in range(2):
-        tile = jnp.where(row == 4 + zl * 2 + w,
+        tile = jnp.where(lane == 4 + zl * 2 + w,
                          0.5 * jnp.sum(dens[pl.ds(w, 1), pl.ds(0, PTS)] * pot[pl.ds(w, 1), pl.ds(0, PTS)]), tile)
     ebuf[plane] = tile
 
@@ -691,10 +692,10 @@
 def finish(pot, total, pot_out, cou_out, exc_out):
     zl = lax.axis_index("wlk") // 4
     pot_out[...] = pot[...]
-    row = lax.broadcasted_iota(jnp.int32, (8, 128), 0)
+    lane = lax.broadcasted_iota(jnp.int32, (1, 128), 1)
     for w in range(2):
-        exc_out[w] = jnp.sum(jnp.where(row == zl * 2 + w, total[...], 0.0)) * (1.0 / 128)
-        cou_out[w] = jnp.sum(jnp.where(row == 4 + zl * 2 + w, total[...], 0.0)) * (1.0 / 128)
+        exc_out[w] = jnp.sum(jnp.where(lane == zl * 2 + w, total[...], 0.0))
+        cou_out[w] = jnp.sum(jnp.where(lane == 4 + zl * 2 + w, total[...], 0.0))
 
 
 def local(green_half, collocation, occupied, kernel):
@@ -703,7 +704,7 @@
     in_vmem, in_smem = pl.BlockSpec(memory_space=vmem), pl.BlockSpec(memory_space=pltpu.SMEM)
     pot, total = pl.pallas_call(
         body,
-        out_shape=(jax.ShapeDtypeStruct((2, PTS), F32), jax.ShapeDtypeStruct((8, 128), F32)),
+        out_shape=(jax.ShapeDtypeStruct((2, PTS), F32), jax.ShapeDtypeStruct((1, 128), F32)),
         in_specs=[any_space] * 4,
         out_specs=(any_space, in_vmem),
         scratch_shapes=[
@@ -724,7 +725,7 @@
             vmem((512, PAD), F32),
             vmem((2, PAD), F32),
             vmem((16, 2, PAD), F32),
-            vmem((32, 8, 128), F32),
+            vmem((32, 1, 128), F32),
             vmem((4, 8, 256), F32),
             vmem((2, ROWS), F32),
             pltpu.SemaphoreType.DMA((8,)),

time: 78.9 us -> 78.5 us (level)
  no operation moved by 1% of the time
where the time goes in v3:
time: 78.5 us; the launch traced here: 78.3 us
  Pallas kernels  77.5 us (99%)
  between operations  0.8 us (1%)
    pallas_call x1, Pallas kernels, local(): pl.pallas_call(body, out_shape=(jax.ShapeDtypeStruct((2, PTS), F32), jax....  76.2 us

profile of v3, /device:TPU:1, one launch (start us, length us, event | category | flops | bytes accessed | tf_op | source)
XLA Modules:
  0.0 78.3 jit_solution(16807543733747573722)
XLA Ops:
  0.6 76.2 %shard_map.67 = (f32[2,600]{1,0:T(2,128)}, f32[1,128]{1,0:T(1,128)}) custom-call(bf16[2,400,2400]{2,1,0:T(8,128)(2,1)} %green.1, bf16[300,600]{1,0:T(8,128)(2,1)} %colloc.1, bf16[400,600]{1,0:T(8,128)(2,1)} %bitcast.1, bf16[600,9600]{1,0:T(8,128)(2,1)} %kmat.1), custom_call_target="tpu_custom_call" | custom-call | tf_op jit(solution)/shard_map/pallas_call | solution.py:705
  76.8 1.3 %shard_map.68 = (f32[2,600]{1,0:T(2,128)}, f32[2]{0:T(128)}, f32[2]{0:T(128)}) custom-call(f32[2,600]{1,0:T(2,128)} %get-tuple-element.5.pot, f32[1,128]{1,0:T(1,128)} %get-tuple-element.6.total), custom_call_target="tpu_custom_call" | custom-call | tf_op jit(solution)/shard_map/pallas_call | solution.py:742
